TPU v7x, 32 devices: a whole 2x2x4 slice. The times are simulated.
32 devices in a mesh: groups: 2 (over y), seq: 4 (over z), heads: 2 (over x), sub: 2 (over core).
Axes of the slice: x: 2, y: 2, z: 4, core: 2. Of those that a mesh axis runs over, the one named last changes fastest.
Arguments:
- queries: bfloat16 [2048, 8192], P(('groups', 'seq', 'sub'), 'heads'), parts along dimension 0, may hold values from -400 to 400
- keys: bfloat16 [2048, 1024], P(('groups', 'seq', 'sub'), 'heads'), parts along dimension 0, may hold values from -6 to 6
- values: bfloat16 [2048, 1024], P(('groups', 'seq', 'sub'), 'heads'), parts along dimension 0, may hold values from -18 to 18
- half_order: int32 [32], P('groups'), parts along dimension 0, may hold values from 0 to 15, as said below
- frame_lengths: int32 [16], P('groups'), parts along dimension 0, may hold values from 1 to 256, 1024 in all
- out_proj: bfloat16 [8192, 4096], P('heads', ('seq', 'sub')), may hold values from -0.09375 to 0.09375
- residual_in: bfloat16 [2048, 4096], P(('groups', 'seq', 'sub'), 'heads'), parts along dimension 0, may hold values from -40 to 40
- norm_gain: float32 [4096], P('heads'), may hold values from 0.5 to 1.5
Outputs:
- attended: bfloat16 [2048, 8192], P(('groups', 'seq', 'sub'), 'heads'), parts along dimension 0
- hidden_state: bfloat16 [2048, 4096], P(('groups', 'seq', 'sub'), 'heads'), parts along dimension 0
- normed: bfloat16 [2048, 4096], P(('groups', 'seq', 'sub'), 'heads'), parts along dimension 0
There are 2 independent parts, one for each index of `groups`. A program takes and returns all parts, laid end to end along the dimension named above; an argument that names none is the same for every part. Nothing has to cross between parts.
Inputs may be any that keep to these rules, and one draw needn't show every extreme that they name: `half_order`: a permutation of 0 to 15.
All inputs are finite; a program needn't handle non-finite values.
Results may differ from a plain program's by a relative error of at most 0.005.
Values may be sent and summed in bfloat16 or wider, within the bound.
A program may use at most 128 MiB of HBM per device.

v0:
```python
import jax
import jax.numpy as jnp
from jax import lax
from jax.sharding import PartitionSpec as P

HEAD_WIDTH = 128
OUT_WIDTH = 4096


def shards(queries, keys, values, half_order, frame_lengths, out_proj, residual_in, norm_gain):
    tok_rows = queries.shape[0]
    kv_local = keys.shape[1] // HEAD_WIDTH
    group_width = queries.shape[1] // keys.shape[1]
    half_rows = tok_rows // 2
    own_index = lax.axis_index("seq") * lax.axis_size("sub") + lax.axis_index("sub")
    table_ids = jnp.arange(half_order.shape[0], dtype=jnp.int32)

    def locate(row_ids):
        matches = (row_ids // half_rows)[:, None] == table_ids[None, :]
        offsets = jnp.sum(jnp.where(matches, half_order[None, :], 0), axis=1)
        return offsets * half_rows + row_ids % half_rows

    query_pos = locate(own_index * tok_rows + jnp.arange(tok_rows, dtype=jnp.int32))
    frame_ends = jnp.cumsum(frame_lengths)
    frame_starts = frame_ends - frame_lengths
    frame_limit = jnp.sum(
        jnp.where(frame_starts[None, :] <= query_pos[:, None], frame_lengths[None, :], 0), axis=1
    )
    query_head_rows = queries.reshape(tok_rows, kv_local, group_width, HEAD_WIDTH)
    score_scale = HEAD_WIDTH ** (-0.5)
    initial = (
        jnp.full((kv_local, group_width, tok_rows), -1e30, jnp.float32),
        jnp.zeros((kv_local, group_width, tok_rows), jnp.float32),
        jnp.zeros((kv_local, group_width, tok_rows, HEAD_WIDTH), jnp.float32),
    )
    key_piece = lax.all_gather(keys, ("seq", "sub"), axis=0, tiled=True)
    value_piece = lax.all_gather(values, ("seq", "sub"), axis=0, tiled=True)
    piece_rows = key_piece.shape[0]
    key_pos = locate(jnp.arange(piece_rows, dtype=jnp.int32))

    def absorb_piece(current):
        running_max, denominator, numerator = current
        key_view = key_piece.reshape(piece_rows, kv_local, HEAD_WIDTH)
        value_view = value_piece.reshape(piece_rows, kv_local, HEAD_WIDTH)
        scores = (
            jnp.einsum(
                "qhgd,khd->hgqk", query_head_rows, key_view, preferred_element_type=jnp.float32
            )
            * score_scale
        )
        visible = key_pos[None, :] < frame_limit[:, None]
        scores = jnp.where(visible, scores, -1e30)
        new_max = jnp.maximum(running_max, jnp.max(scores, axis=-1))
        weights = jnp.where(visible, jnp.exp(scores - new_max[..., None]), 0.0)
        denominator = jnp.sum(weights, axis=-1)
        product = jnp.einsum(
            "hgqk,khd->hgqd",
            weights.astype(jnp.bfloat16),
            value_view,
            preferred_element_type=jnp.float32,
        )
        numerator = product
        return (new_max, denominator, numerator)

    running_max, denominator, numerator = lax.cond(
        jnp.min(key_pos) < jnp.max(frame_limit), absorb_piece, lambda current: current, initial
    )
    result = numerator / denominator[..., None]
    attended = (
        jnp.transpose(result, (2, 0, 1, 3))
        .reshape(tok_rows, kv_local * group_width * HEAD_WIDTH)
        .astype(jnp.bfloat16)
    )
    gathered = lax.all_gather(attended, ("seq", "sub"), axis=0, tiled=True)
    column_terms = jnp.dot(gathered, out_proj, preferred_element_type=jnp.float32)
    head_terms = lax.all_to_all(
        column_terms.astype(jnp.bfloat16), ("seq", "sub"), split_axis=0, concat_axis=1, tiled=True
    )
    projected = lax.psum_scatter(head_terms, "heads", scatter_dimension=1, tiled=True).astype(
        jnp.float32
    )
    hidden_state = (residual_in.astype(jnp.float32) + projected).astype(jnp.bfloat16)
    widened = hidden_state.astype(jnp.float32)
    energy = lax.psum(jnp.sum(widened * widened, axis=1), "heads") / OUT_WIDTH
    normed = (widened * lax.rsqrt(energy + 1e-06)[:, None] * norm_gain[None, :]).astype(
        jnp.bfloat16
    )
    return (attended, hidden_state, normed)


def solution(mesh):
    in_specs = (
        P(("groups", "seq", "sub"), "heads"),
        P(("groups", "seq", "sub"), "heads"),
        P(("groups", "seq", "sub"), "heads"),
        P("groups"),
        P("groups"),
        P("heads", ("seq", "sub")),
        P(("groups", "seq", "sub"), "heads"),
        P("heads"),
    )
    out_specs = (
        P(("groups", "seq", "sub"), "heads"),
        P(("groups", "seq", "sub"), "heads"),
        P(("groups", "seq", "sub"), "heads"),
    )
    return jax.shard_map(shards, mesh=mesh, in_specs=in_specs, out_specs=out_specs, check_vma=False)
```

profile of v0, /device:TPU:0, one launch (start us, length us, event | category | flops | bytes accessed | tf_op | source)
XLA Modules:
  0.0 242.6 jit_solution(11686447598363568925)
XLA Ops:
  7.2 0.0 all-gather.4.cloned.1.call-start
  7.2 0.7 all-gather.4.cloned.1.call-update
  7.9 0.0 all-gather.6.cloned.1.call-start
  7.9 0.7 all-gather.6.cloned.1.call-update
  8.6 0.0 all-gather.8.cloned.1.call-start
  8.7 0.8 reduce-window.9
  9.5 0.7 select_reduce_fusion.1
  10.3 0.7 bitcast_subtract_fusion
  11.0 0.7 select_reduce_fusion.2
  11.7 0.6 reduce_max.18
  12.3 0.7 select_reduce_fusion
  13.1 0.6 fusion.26
  15.0 19.6 %all-gather.4.cloned.1.call-done = bf16[1024,512]{1,0:T(8,128)(2,1)} async-done(((bf16[128,512]{1,0:T(8,128)(2,1)}), bf16[1024,512]{1,0:T(8,128)(2,1)}) %all-gather.4.cloned.1.call-update) | async-done | bytes 1048592 | tf_op jit(solution)/shard_map/all_gather | solution.py:36
  34.6 23.5 %all-gather.6.cloned.1.call-done = bf16[1024,512]{1,0:T(8,128)(2,1)} async-done(((bf16[128,512]{1,0:T(8,128)(2,1)}), bf16[1024,512]{1,0:T(8,128)(2,1)}) %all-gather.6.cloned.1.call-update) | async-done | bytes 1048592 | tf_op jit(solution)/shard_map/all_gather | solution.py:37
  58.0 27.6 %conditional.1 = (f32[4,8,128]{2,1,0:T(8,128)S(1)}, f32[4,8,128,128]{3,2,1,0:T(8,128)S(1)}) conditional(s32[]{:T(128)} %convert_element_type.33, () %tuple.16, (s32[1024]{0:T(1024)S(1)}, s32[128]{0:T(128)S(1)}, bf16[1024,512]{1,0:T(8,128)(2,1)}, bf16[128,4096]{1,0:T(8,128)(2,1)}, bf16[1024,512]{1,0:T(8,128)(2,1)}) %tuple.17), branch_computations={%region_6.7_spmd, %region_7.10_spmd} | conditional | flops 2202136576 | bytes 66687532 | solution.py:65
  58.0 0.0 copy-start.1
  58.0 0.2 broadcast_compare_fusion
  58.3 1.4 reshape.102
  59.7 1.5 copy.31
  61.2 7.2 %fusion = (f32[4,8,128]{2,1,0:T(8,128)S(1)}, f32[4,1024,128,8]{2,1,3,0:T(8,128)}) fusion(pred[128,1024]{0,1:T(8,128)(4,1)S(1)} %broadcast_compare_fusion, bf16[128,4,8,128]{3,2,1,0:T(8,128)(2,1)S(1)} %bitcast.38, bf16[1024,4,128,1]{2,1,0,3:T(4,128)(2,1)S(1)} %bitcast.37), kind=kOutput, calls=%fused_computation.2 | convolution fusion | flops 1086320640 | bytes 19021824 | tf_op jit(solution)/shard_map/cond/branch_1_fun/qhgd,khd->hgqk/dot_general | solution.py:46
  68.4 0.0 copy-done.1
  68.4 0.3 reshape.104
  68.7 9.0 %fusion.3 = f32[4,8,128,128]{3,2,1,0:T(8,128)S(1)} fusion(f32[4,1024,128,8]{2,1,3,0:T(8,128)} %get-tuple-element.30, f32[4,8,128]{2,1,0:T(8,128)S(1)} %broadcast_maximum_fusion, pred[128,1024]{0,1:T(8,128)(4,1)S(1)} %broadcast_compare_fusion, bf16[1024,4,128,1]{2,1,0,3:T(4,128)(2,1)S(1)} %bitcast.41), kind=kOutput, calls=%fused_computation.5 | convolution fusion | flops 1094713344 | bytes 20070400 | tf_op jit(solution)/shard_map/cond/branch_1_fun/hgqk,khd->hgqd/dot_general | solution.py:56
  77.7 8.0 %fusion.2 = f32[4,8,128]{2,1,0:T(8,128)S(1)} fusion(f32[4,1024,128,8]{2,1,3,0:T(8,128)} %get-tuple-element.30, f32[4,8,128]{2,1,0:T(8,128)S(1)} %broadcast_maximum_fusion, pred[128,1024]{0,1:T(8,128)(4,1)S(1)} %broadcast_compare_fusion), kind=kLoop, calls=%fused_computation.4 | loop fusion | flops 20967424 | bytes 16941056 | tf_op jit(solution)/shard_map/cond/branch_1_fun/reduce_sum | solution.py:55
  85.6 0.7 fusion.16
  86.4 0.7 copy.22
  87.1 1.4 copy.45
  88.5 0.0 all-gather.8.cloned.1.call-update
  88.5 0.0 copy-start.2
  88.5 0.0 copy-start.3
  88.5 0.0 reduce-scatter.2.cloned.1.call-start
  88.6 81.7 %all-gather.8.cloned.1.call-done = bf16[1024,4096]{1,0:T(8,128)(2,1)} async-done(((bf16[128,4096]{1,0:T(8,128)(2,1)}), bf16[1024,4096]{1,0:T(8,128)(2,1)}) %all-gather.8.cloned.1.call-update) | async-done | bytes 8388624 | tf_op jit(solution)/shard_map/all_gather | solution.py:74
  170.3 9.1 %convolution_convert_fusion = bf16[1024,512]{1,0:T(8,128)(2,1)S(1)} fusion(bf16[1024,4096]{1,0:T(8,128)(2,1)} %all-gather.8.cloned.1.call-done, bf16[4096,512]{1,0:T(8,128)(2,1)} %param.15), kind=kOutput, calls=%fused_computation.17 | convolution fusion | flops 4295491584 | bytes 13631488 | tf_op jit(solution)/shard_map/dot_general | solution.py:75
  179.4 29.0 %all_to_all.19 = bf16[8,128,512]{2,1,0:T(8,128)(2,1)S(1)} all-to-all(bf16[8,128,512]{2,1,0:T(8,128)(2,1)S(1)} %bitcast.40), channel_id=1, replica_groups=mesh['groups'=2,'seq'=4,'heads'=2,'sub'=2] {'seq','sub'}, dimensions={0} | all-to-all | bytes 2097152 | tf_op jit(solution)/shard_map/all_to_all | solution.py:76
  208.3 1.1 copy.32
  209.4 0.0 reduce-scatter.2.cloned.1.call-update
  209.5 19.4 %reduce-scatter.2.cloned.1.call-done = bf16[128,2048]{1,0:T(8,128)(2,1)} async-done(((bf16[128,4096]{1,0:T(8,128)(2,1)}), bf16[128,2048]{1,0:T(8,128)(2,1)}) %reduce-scatter.2.cloned.1.call-update) | async-done | bytes 524304 | tf_op jit(solution)/shard_map/reduce_scatter | solution.py:79
  228.9 0.0 copy-done.2
  228.9 1.3 fusion.13
  230.2 0.0 copy-start
  230.2 4.9 %psum.7 = f32[128]{0:T(128)S(1)} all-reduce(f32[128]{0:T(128)S(1)} %get-tuple-element.25), channel_id=1, replica_groups=mesh['groups'=2,'seq'=4,'heads'=2,'sub'=2] {'heads'}, use_global_device_ids=true, to_apply=%region_12.13 | all-reduce | flops 128 | bytes 1024 | tf_op jit(solution)/shard_map/psum | solution.py:84
  235.1 0.0 copy-done.3
  235.1 1.0 fusion.15
  236.1 0.0 copy-done
  (5 shorter events, 0.0 us)
Async XLA Ops:
  7.2 27.4 %all-gather.4.cloned.1.call-start = ((), (), s32[]{:S(2)}) async-start(), calls=%async_computation.2 | async-start | bytes 1179648 | tf_op jit(solution)/shard_map/all_gather | solution.py:36
  7.9 50.1 %all-gather.6.cloned.1.call-start = ((), (), s32[]{:S(2)}) async-start(), calls=%async_computation.3 | async-start | bytes 1179648 | tf_op jit(solution)/shard_map/all_gather | solution.py:37
  8.6 161.6 %all-gather.8.cloned.1.call-start = ((), (), s32[]{:S(2)}) async-start(), calls=%async_computation.4 | async-start | bytes 9437184 | tf_op jit(solution)/shard_map/all_gather | solution.py:74
  58.0 10.4 %copy-start.1 = (bf16[1024,512]{1,0:T(8,128)(2,1)S(1)}, bf16[1024,512]{1,0:T(8,128)(2,1)}, u32[]{:S(2)}) copy-start(bf16[1024,512]{1,0:T(8,128)(2,1)} %get-tuple-element.15) | copy-start | bytes 3145732 | tf_op jit(solution)/shard_map/cond
  88.5 140.4 %copy-start.2 = (bf16[128,2048]{1,0:T(8,128)(2,1)S(1)}, bf16[128,2048]{1,0:T(8,128)(2,1)}, u32[]{:S(2)}) copy-start(bf16[128,2048]{1,0:T(8,128)(2,1)} %param.16) | copy-start | bytes 1572868
  88.5 146.6 %copy-start.3 = (f32[2048]{0:T(1024)S(1)}, f32[2048]{0:T(1024)}, u32[]{:S(2)}) copy-start(f32[2048]{0:T(1024)} %param.17) | copy-start | bytes 24580
  88.5 140.3 %reduce-scatter.2.cloned.1.call-start = ((), (), s32[]{:S(2)}) async-start(), calls=%async_computation.5 | async-start | bytes 1572864 | tf_op jit(solution)/shard_map/reduce_scatter | solution.py:79
  230.2 5.9 %copy-start = (bf16[128,2048]{1,0:T(8,128)(2,1)}, bf16[128,2048]{1,0:T(8,128)(2,1)S(1)}, u32[]{:S(2)}) copy-start(bf16[128,2048]{1,0:T(8,128)(2,1)S(1)} %get-tuple-element.26) | copy-start | bytes 1572868
Sparse Core Ops, SparseCore 0:
  9.6 24.9 all-gather.3
  36.2 21.8 all-gather.5
  88.6 81.6 all-gather.7
  209.6 19.2 reduce-scatter.1
where the time goes:
time: 243 us
  waiting for transfers between devices  146 us (60%)
  blocking collectives  33.9 us (14%)
  matrix products  25.2 us (10%)
  other arithmetic  16.2 us (7%)
  between operations  15.1 us (6%)
  local copies, waits for them, and re-layouts  6.39 us (3%)
    all_gather x1, waiting for transfers between devices, shards(): gathered = lax.all_gather(attended, ('seq', 'sub'), axis=0, tiled=True)  81.7 us
    all_to_all x1, blocking collectives, shards(): lax.all_to_all(column_terms.astype(jnp.bfloat16), ('seq', 'sub'), split_a...  29 us
    all_gather x1, waiting for transfers between devices, shards(): value_piece = lax.all_gather(values, ('seq', 'sub'), axis=0, tiled=True)  23.5 us
    all_gather x1, waiting for transfers between devices, shards(): key_piece = lax.all_gather(keys, ('seq', 'sub'), axis=0, tiled=True)  19.6 us
    reduce_scatter x1, waiting for transfers between devices, shards(): lax.psum_scatter(head_terms, 'heads', scatter_dimension=1, tiled=True)  19.4 us
    dot_general x1, matrix products, shards(): jnp.dot(gathered, out_proj, preferred_element_type=jnp.float32)  9.05 us
    dot_general x1, matrix products, absorb_piece(): jnp.einsum('hgqk,khd->hgqd', weights.astype(jnp.bfloat16), value_view, pr...  8.97 us
    reduce_sum x1, other arithmetic, absorb_piece(): denominator = jnp.sum(weights, axis=-1)  7.98 us
  transfers between devices with their start and end apart: 4, of which 4 were waited for; matrix products, arithmetic and copies ran while one was open for 2% of the time, Pallas kernels for 0%

commit v1 on v0

--- a/solution.py
+++ b/solution.py
@@ -33,8 +33,11 @@
         jnp.zeros((kv_local, group_width, tok_rows), jnp.float32),
         jnp.zeros((kv_local, group_width, tok_rows, HEAD_WIDTH), jnp.float32),
     )
-    key_piece = lax.all_gather(keys, ("seq", "sub"), axis=0, tiled=True)
-    value_piece = lax.all_gather(values, ("seq", "sub"), axis=0, tiled=True)
+    key_piece, value_piece = jnp.split(
+        lax.all_gather(jnp.concatenate([keys, values], axis=1), ("seq", "sub"), axis=0, tiled=True),
+        [keys.shape[1]],
+        axis=1,
+    )
     piece_rows = key_piece.shape[0]
     key_pos = locate(jnp.arange(piece_rows, dtype=jnp.int32))
 

time: 243 us -> 228 us (0.938)
  waiting for transfers between devices: 146 us -> 128 us
    all_gather x2 -> x1, waiting for transfers between devices: 43 us -> 27.1 us  [shards(): lax.all_gather(jnp.concatenate([keys, values], axis=1), ('seq', 'sub'), a...]
  transfers between devices with their start and end apart: 4 -> 3, of which waited for: 4 -> 3; matrix products, arithmetic and copies ran while one was open for 2% -> 2% of each run, Pallas kernels for 0% -> 0%
where the time goes in v1:
time: 228 us; the launch traced here: 227 us
  waiting for transfers between devices  128 us (56%)
  blocking collectives  33.9 us (15%)
  matrix products  25.2 us (11%)
  other arithmetic  17 us (7%)
  between operations  15.1 us (7%)
  local copies, waits for them, and re-layouts  8.43 us (4%)
    all_gather x1, waiting for transfers between devices, shards(): gathered = lax.all_gather(attended, ('seq', 'sub'), axis=0, tiled=True)  81.1 us
    all_to_all x1, blocking collectives, shards(): lax.all_to_all(column_terms.astype(jnp.bfloat16), ('seq', 'sub'), split_a...  29 us
    all_gather x1, waiting for transfers between devices, shards(): lax.all_gather(jnp.concatenate([keys, values], axis=1), ('seq', 'sub'), a...  27.1 us
    reduce_scatter x1, waiting for transfers between devices, shards(): lax.psum_scatter(head_terms, 'heads', scatter_dimension=1, tiled=True)  19.4 us
    dot_general x1, matrix products, shards(): jnp.dot(gathered, out_proj, preferred_element_type=jnp.float32)  9.05 us
    dot_general x1, matrix products, absorb_piece(): jnp.einsum('hgqk,khd->hgqd', weights.astype(jnp.bfloat16), value_view, pr...  8.92 us
    reduce_sum x1, other arithmetic, absorb_piece(): denominator = jnp.sum(weights, axis=-1)  7.98 us
    dot_general x1, matrix products, absorb_piece(): jnp.einsum('qhgd,khd->hgqk', query_head_rows, key_view, preferred_element...  7.26 us
  transfers between devices with their start and end apart: 3, of which 3 were waited for; matrix products, arithmetic and copies ran while one was open for 2% of the time, Pallas kernels for 0%

profile of v1, /device:TPU:0, one launch (start us, length us, event | category | flops | bytes accessed | tf_op | source)
XLA Modules:
  0.0 227.5 jit_solution(3750876178591853679)
XLA Ops:
  7.2 0.0 all-gather.3.cloned.1.call-start
  7.2 1.0 copy.28
  8.2 1.0 copy.29
  9.3 0.7 pad_maximum_fusion
  10.0 0.0 all-gather.3.cloned.1.call-update
  10.0 0.0 all-gather.5.cloned.1.call-start
  10.1 0.8 reduce-window.9
  10.9 0.7 select_reduce_fusion.1
  11.7 0.7 bitcast_subtract_fusion
  12.3 0.7 select_reduce_fusion.2
  13.1 0.6 reduce_max.18
  13.7 0.7 select_reduce_fusion
  14.5 0.6 fusion.24
  16.4 27.1 %all-gather.3.cloned.1.call-done = bf16[1024,1024]{0,1:T(8,128)(2,1)} async-done(((bf16[128,1024]{0,1:T(8,128)(2,1)}), bf16[1024,1024]{0,1:T(8,128)(2,1)}) %all-gather.3.cloned.1.call-update) | async-done | bytes 2097168 | tf_op jit(solution)/shard_map/all_gather | solution.py:37
  43.5 27.6 %conditional.1 = (f32[4,8,128]{2,1,0:T(8,128)S(1)}, f32[4,8,128,128]{3,2,1,0:T(8,128)S(1)}) conditional(s32[]{:T(128)} %convert_element_type.33, () %tuple.16, (s32[1024]{0:T(1024)S(1)}, s32[128]{0:T(128)S(1)}, bf16[1024,1024]{0,1:T(8,128)(2,1)}, bf16[128,4096]{1,0:T(8,128)(2,1)}) %tuple.17), branch_computations={%region_6.7_spmd, %region_7.10_spmd} | conditional | flops 2202136576 | bytes 62493200 | solution.py:68
  43.5 0.2 broadcast_compare_fusion
  43.7 1.7 fusion.26
  45.4 1.5 copy.39
  46.9 7.3 %fusion = (f32[4,8,128]{2,1,0:T(8,128)S(1)}, f32[4,1024,128,8]{2,1,3,0:T(8,128)}) fusion(pred[128,1024]{0,1:T(8,128)(4,1)S(1)} %broadcast_compare_fusion, bf16[1024,4,128,1]{0,2,3,1:T(8,128)(2,1)S(1)} %bitcast.48, bf16[128,4,8,128]{3,2,1,0:T(8,128)(2,1)S(1)} %bitcast.47), kind=kOutput, calls=%fused_computation.2 | convolution fusion | flops 1086320640 | bytes 19021824 | tf_op jit(solution)/shard_map/cond/branch_1_fun/qhgd,khd->hgqk/dot_general | solution.py:49
  54.2 8.9 %fusion.3 = f32[4,8,128,128]{3,2,1,0:T(8,128)S(1)} fusion(bf16[1024,4,128,1]{0,2,3,1:T(8,128)(2,1)S(1)} %bitcast.51, f32[4,1024,128,8]{2,1,3,0:T(8,128)} %get-tuple-element.32, f32[4,8,128]{2,1,0:T(8,128)S(1)} %broadcast_maximum_fusion, pred[128,1024]{0,1:T(8,128)(4,1)S(1)} %broadcast_compare_fusion), kind=kOutput, calls=%fused_computation.5 | convolution fusion | flops 1094713344 | bytes 20070400 | tf_op jit(solution)/shard_map/cond/branch_1_fun/hgqk,khd->hgqd/dot_general | solution.py:59
  63.1 8.0 %fusion.2 = f32[4,8,128]{2,1,0:T(8,128)S(1)} fusion(f32[4,1024,128,8]{2,1,3,0:T(8,128)} %get-tuple-element.32, f32[4,8,128]{2,1,0:T(8,128)S(1)} %broadcast_maximum_fusion, pred[128,1024]{0,1:T(8,128)(4,1)S(1)} %broadcast_compare_fusion), kind=kLoop, calls=%fused_computation.4 | loop fusion | flops 20967424 | bytes 16941056 | tf_op jit(solution)/shard_map/cond/branch_1_fun/reduce_sum | solution.py:58
  71.1 0.7 fusion.14
  71.8 0.7 copy.30
  72.5 1.4 copy.47
  73.9 0.0 all-gather.5.cloned.1.call-update
  73.9 0.0 copy-start.1
  74.0 0.0 copy-start.2
  74.0 0.0 reduce-scatter.2.cloned.1.call-start
  74.0 81.1 %all-gather.5.cloned.1.call-done = bf16[1024,4096]{1,0:T(8,128)(2,1)} async-done(((bf16[128,4096]{1,0:T(8,128)(2,1)}), bf16[1024,4096]{1,0:T(8,128)(2,1)}) %all-gather.5.cloned.1.call-update) | async-done | bytes 8388624 | tf_op jit(solution)/shard_map/all_gather | solution.py:77
  155.1 9.0 %convolution_convert_fusion = bf16[1024,512]{1,0:T(8,128)(2,1)S(1)} fusion(bf16[1024,4096]{1,0:T(8,128)(2,1)} %all-gather.5.cloned.1.call-done, bf16[4096,512]{1,0:T(8,128)(2,1)} %param.15), kind=kOutput, calls=%fused_computation.15 | convolution fusion | flops 4295491584 | bytes 13631488 | tf_op jit(solution)/shard_map/dot_general | solution.py:78
  164.2 29.0 %all_to_all.19 = bf16[8,128,512]{2,1,0:T(8,128)(2,1)S(1)} all-to-all(bf16[8,128,512]{2,1,0:T(8,128)(2,1)S(1)} %bitcast.50), channel_id=1, replica_groups=mesh['groups'=2,'seq'=4,'heads'=2,'sub'=2] {'seq','sub'}, dimensions={0} | all-to-all | bytes 2097152 | tf_op jit(solution)/shard_map/all_to_all | solution.py:79
  193.2 1.1 copy.40
  194.3 0.0 reduce-scatter.2.cloned.1.call-update
  194.3 19.4 %reduce-scatter.2.cloned.1.call-done = bf16[128,2048]{1,0:T(8,128)(2,1)} async-done(((bf16[128,4096]{1,0:T(8,128)(2,1)}), bf16[128,2048]{1,0:T(8,128)(2,1)}) %reduce-scatter.2.cloned.1.call-update) | async-done | bytes 524304 | tf_op jit(solution)/shard_map/reduce_scatter | solution.py:82
  213.7 0.0 copy-done.1
  213.7 1.3 fusion.11
  215.0 0.0 copy-start
  215.0 4.9 %psum.7 = f32[128]{0:T(128)S(1)} all-reduce(f32[128]{0:T(128)S(1)} %get-tuple-element.25), channel_id=1, replica_groups=mesh['groups'=2,'seq'=4,'heads'=2,'sub'=2] {'heads'}, use_global_device_ids=true, to_apply=%region_12.13 | all-reduce | flops 128 | bytes 1024 | tf_op jit(solution)/shard_map/psum | solution.py:87
  220.0 0.0 copy-done.2
  220.0 1.0 fusion.13
  221.0 0.0 copy-done
  (5 shorter events, 0.0 us)
Async XLA Ops:
  7.2 36.3 %all-gather.3.cloned.1.call-start = ((), (), s32[]{:S(2)}) async-start(), calls=%async_computation.2 | async-start | bytes 2359296 | tf_op jit(solution)/shard_map/all_gather | solution.py:37
  10.0 145.1 %all-gather.5.cloned.1.call-start = ((), (), s32[]{:S(2)}) async-start(), calls=%async_computation.3 | async-start | bytes 9437184 | tf_op jit(solution)/shard_map/all_gather | solution.py:77
  73.9 139.8 %copy-start.1 = (bf16[128,2048]{1,0:T(8,128)(2,1)S(1)}, bf16[128,2048]{1,0:T(8,128)(2,1)}, u32[]{:S(2)}) copy-start(bf16[128,2048]{1,0:T(8,128)(2,1)} %param.16) | copy-start | bytes 1572868
  74.0 146.0 %copy-start.2 = (f32[2048]{0:T(1024)S(1)}, f32[2048]{0:T(1024)}, u32[]{:S(2)}) copy-start(f32[2048]{0:T(1024)} %param.17) | copy-start | bytes 24580
  74.0 139.7 %reduce-scatter.2.cloned.1.call-start = ((), (), s32[]{:S(2)}) async-start(), calls=%async_computation.4 | async-start | bytes 1572864 | tf_op jit(solution)/shard_map/reduce_scatter | solution.py:82
  215.0 5.9 %copy-start = (bf16[128,2048]{1,0:T(8,128)(2,1)}, bf16[128,2048]{1,0:T(8,128)(2,1)S(1)}, u32[]{:S(2)}) copy-start(bf16[128,2048]{1,0:T(8,128)(2,1)S(1)} %get-tuple-element.26) | copy-start | bytes 1572868
Sparse Core Ops, SparseCore 0:
  10.1 33.3 all-gather.2
  74.1 81.0 all-gather.4
  194.4 19.2 reduce-scatter.1
